TPU v7x, 32 devices: a whole 2x2x4 slice. The times are simulated.
32 devices in a mesh: gz: 8 (over z, y), pa: 4 (over x, core).
Axes of the slice: x: 2, y: 2, z: 4, core: 2. Of those that a mesh axis runs over, the one named last changes fastest.
Arguments:
- density: bfloat16 [64, 1024, 1024], P('gz', 'pa'), may hold values from -6 to 6
- green: float32 [128, 1024, 1024], P('gz', 'pa'), may hold values from 0.1 to 3
Outputs:
- potential: float32 [64, 1024, 1024], P('gz', 'pa')
All inputs are finite; a program needn't handle non-finite values.
Results may differ from a plain program's by a relative error of at most 0.02.
Values may be sent and summed in bfloat16 or wider, within the bound.
A program may use at most 192 MiB of HBM per device.

v0:
```python
import math

import jax
import jax.numpy as jnp
from jax import lax
from jax.experimental import pallas as pl
from jax.experimental.pallas import tpu as pltpu
from jax.sharding import PartitionSpec as P

BF = jnp.bfloat16
F32 = jnp.float32
CHUNKS = 2


def cas_table(rows, cols, length):
    product = rows[:, None] * cols[None, :] % length
    angle = product.astype(F32) * (2.0 * math.pi / length)
    return (jnp.cos(angle) + jnp.sin(angle)).astype(BF)


def square_table(n):
    index = jnp.arange(n, dtype=jnp.int32)
    return cas_table(index, index, n)


def cost(flops, *arrays):
    size = sum(math.prod(a.shape) * a.dtype.itemsize for a in arrays)
    return pl.CostEstimate(flops=flops, bytes_accessed=size, transcendentals=0)


def dot(a, b):
    return jnp.dot(a, b, preferred_element_type=F32)


def dot_t(a, b):
    return lax.dot_general(a, b, (((1,), (1,)), ((), ())), preferred_element_type=F32)


def on_rank(body, grid, in_specs, out_specs, out_shape, cost_estimate, **more):
    spec = pltpu.PrefetchScalarGridSpec(
        num_scalar_prefetch=1, grid=grid, in_specs=in_specs, out_specs=out_specs
    )
    return pl.pallas_call(
        lambda r, *refs: body(*refs),
        grid_spec=spec,
        out_shape=out_shape,
        cost_estimate=cost_estimate,
        **more,
    )


def green_piece(green, rank, step, groups):
    k, v, u = green.shape
    share = v // groups
    cut = math.gcd(k, 4)
    pieces = green.reshape(k, groups, share, u)

    def body(g_ref, o_ref):
        o_ref[...] = g_ref[:, 0].astype(BF)

    out = jax.ShapeDtypeStruct((k, share, u), BF)
    return on_rank(
        body,
        (k // cut,),
        [pl.BlockSpec((cut, 1, share, u), lambda i, r: (i, lax.rem(r[0] + step, groups), 0, 0))],
        pl.BlockSpec((cut, share, u), lambda i, r: (i, 0, 0)),
        out,
        cost(0, out, out, out),
    )(rank, pieces)


def shift(a, axis, step):
    n = lax.axis_size(axis)
    return lax.ppermute(a, axis, [(i, (i + step) % n) for i in range(n)])


def y_forward(density, table, pencils):
    z, x, y = density.shape
    block = y // pencils

    def body(d_ref, t_ref, o_ref):
        for p in range(pencils):
            rows = t_ref[p * block : (p + 1) * block, :]
            o_ref[p, 0] = dot_t(rows, d_ref[0]).astype(BF)

    out = jax.ShapeDtypeStruct((pencils, z, block, x), BF)
    return pl.pallas_call(
        body,
        grid=(z,),
        in_specs=[
            pl.BlockSpec((1, x, y), lambda i: (i, 0, 0)),
            pl.BlockSpec((y, y), lambda i: (0, 0)),
        ],
        out_specs=pl.BlockSpec((pencils, 1, block, x), lambda i: (0, i, 0, 0)),
        out_shape=out,
        cost_estimate=cost(2 * z * x * y * y, density, table, out),
        name="y_forward",
    )(density, table)


def x_forward(moved, table, groups):
    pencils, z, v, x = moved.shape
    u = pencils * x
    share = v // groups

    def body(m_ref, t_ref, o_ref):
        total = dot(m_ref[0, 0], t_ref[0:x, :])
        for p in range(1, pencils):
            total += dot(m_ref[p, 0], t_ref[p * x : (p + 1) * x, :])
        total = total.astype(BF)
        for j in range(groups):
            o_ref[j, 0] = total[j * share : (j + 1) * share, :]

    out = jax.ShapeDtypeStruct((groups, z, share, u), BF)
    return pl.pallas_call(
        body,
        grid=(z,),
        in_specs=[
            pl.BlockSpec((pencils, 1, v, x), lambda i: (0, i, 0, 0)),
            pl.BlockSpec((u, u), lambda i: (0, 0)),
        ],
        out_specs=pl.BlockSpec((groups, 1, share, u), lambda i: (0, i, 0, 0)),
        out_shape=out,
        cost_estimate=cost(2 * z * v * u * u, moved, table, out),
        name="x_forward",
    )(moved, table)


def z_weight(planes, greens, table, chunks):
    z, v, u = planes.shape
    groups = len(greens)
    part = greens[0].shape[0]
    k = part * groups
    depth = z // groups // chunks
    if v % 8:
        green = jnp.concatenate(greens, axis=0)
        spec = jnp.einsum("kz,zvu->kvu", table, planes, preferred_element_type=F32)
        weighted = (green.astype(F32) * spec).astype(BF)
        back = jnp.einsum("kz,kvu->zvu", table, weighted, preferred_element_type=F32).astype(BF)
        back = back.reshape(groups, chunks, depth, v, u)
        return [back[:, c] for c in range(chunks)]
    lanes = min(u, 512)
    rows = 16 if v % 16 == 0 else 8
    row = jnp.arange(8, dtype=jnp.int32)

    def widen(t):
        same = (jnp.arange(8 * t.shape[0]) % 8)[:, None] == (jnp.arange(8 * t.shape[1]) % 8)[None]
        return jnp.where(same, jnp.repeat(jnp.repeat(t, 8, axis=0), 8, axis=1), 0).astype(BF)

    wide = widen(table)
    tall = widen(table.T)

    def body(s_ref, *refs):
        g_refs, (w_ref, t_ref), o_refs = refs[:groups], refs[groups : groups + 2], refs[groups + 2 :]
        for i in range(0, rows, 8):
            flat = s_ref[:, i : i + 8, :].astype(F32).reshape(z * 8, lanes).astype(BF)
            spec = dot(w_ref[...], flat)
            weight = jnp.concatenate(
                [g[:, i : i + 8, :].astype(F32).reshape(part * 8, lanes) for g in g_refs], axis=0
            )
            back = dot(t_ref[...], (spec * weight).astype(BF))
            back = back.reshape(groups, chunks, depth, 8, lanes).astype(BF)
            for c in range(chunks):
                o_refs[c][:, :, i : i + 8, :] = back[:, c]

    out = jax.ShapeDtypeStruct((groups, depth, v, u), BF)
    at = lambda i, j: (0, i, j)
    whole = lambda i, j: (0, 0)
    return pl.pallas_call(
        body,
        grid=(v // rows, u // lanes),
        in_specs=[
            pl.BlockSpec((z, rows, lanes), at),
            *[pl.BlockSpec((part, rows, lanes), at)] * groups,
            pl.BlockSpec((k * 8, z * 8), whole),
            pl.BlockSpec((z * 8, k * 8), whole),
        ],
        out_specs=[pl.BlockSpec((groups, depth, rows, lanes), lambda i, j: (0, 0, i, j))] * chunks,
        out_shape=[out] * chunks,
        compiler_params=pltpu.CompilerParams(vmem_limit_bytes=60 * 2**20),
        cost_estimate=cost(32 * z * k * v * u, planes, *greens, planes),
        name="z_weight",
    )(planes, *greens, wide, tall)


def x_inverse(back, table, rank, step, pencils):
    groups, z, share, u = back.shape
    v = groups * share
    x = u // pencils

    def body(b_ref, t_ref, o_ref):
        rows = jnp.concatenate([b_ref[j, 0] for j in range(groups)], axis=0)
        o_ref[0] = dot_t(t_ref[...], rows).astype(BF)

    out = jax.ShapeDtypeStruct((z, x, v), BF)
    return on_rank(
        body,
        (z,),
        [
            pl.BlockSpec((groups, 1, share, u), lambda i, r: (0, i, 0, 0)),
            pl.BlockSpec((x, u), lambda i, r: (lax.rem(r[0] + step, pencils), 0)),
        ],
        pl.BlockSpec((1, x, v), lambda i, r: (i, 0, 0)),
        out,
        cost(2 * z * v * u * x, back, out),
    )(rank, back, table)


def y_inverse(returned, table, rank, scale, total, z_all, first):
    pencils = len(returned)
    z, x, v = returned[0].shape
    y = pencils * v

    def body(*refs):
        r_refs, t_refs, o_ref = refs[:pencils], refs[pencils : 2 * pencils], refs[-1]
        acc = dot(r_refs[0][0], t_refs[0][...])
        for p in range(1, pencils):
            acc += dot(r_refs[p][0], t_refs[p][...])
        o_ref[0] = acc * scale

    def rows_of(s):
        return lambda i, r: (lax.rem(r[0] + pencils - s, pencils), 0)

    specs = [pl.BlockSpec((1, x, v), lambda i, r: (i, 0, 0))] * pencils
    specs += [pl.BlockSpec((v, y), rows_of(s)) for s in range(pencils)]
    operands = [*returned, *[table] * pencils]
    aliases = {}
    if total is not None:
        aliases = {1 + len(operands): 0}
        specs.append(pl.BlockSpec(memory_space=pl.ANY))
        operands.append(total)
    return on_rank(
        body,
        (z,),
        specs,
        pl.BlockSpec((1, x, y), lambda i, r: (i + first, 0, 0)),
        jax.ShapeDtypeStruct((z_all, x, y), F32),
        cost(2 * z * x * y * y, *returned, *returned, *returned),
        input_output_aliases=aliases,
    )(rank, *operands)


def exchange(a, axis):
    return lax.all_to_all(a, axis, split_axis=0, concat_axis=0, tiled=True)


def staged(density, green):
    z_slab, _, y_cells = density.shape
    k_block, y_local, x_cells = green.shape
    groups = lax.axis_size("gz")
    pencils = lax.axis_size("pa")
    z_cells = z_slab * groups
    z_freqs = k_block * groups
    share = y_local // groups
    g_rank = lax.axis_index("gz").astype(jnp.int32)
    p_rank = lax.axis_index("pa").astype(jnp.int32)
    g_me, p_me = g_rank.reshape(1), p_rank.reshape(1)
    greens = []
    for s in [*range(1, groups), 0]:
        piece = green_piece(green, g_me, s, groups)
        if s:
            piece = shift(piece, "gz", s)
        greens.append(piece)
    order = jnp.array([*range(1, groups), 0], dtype=jnp.int32)
    sources = (g_rank - order) % groups
    f_index = (sources[:, None] * k_block + jnp.arange(k_block, dtype=jnp.int32)).reshape(-1)
    cas_y = square_table(y_cells)
    cas_x = cas_y if x_cells == y_cells else square_table(x_cells)
    cas_m = cas_table(f_index, jnp.arange(z_cells, dtype=jnp.int32), z_freqs)
    moved = y_forward(density, cas_y, pencils)
    moved = exchange(moved, "pa")
    planes = x_forward(moved, cas_x, groups)
    planes = exchange(planes, "gz").reshape(z_cells, share, x_cells)
    chunks = math.gcd(z_slab, CHUNKS)
    scale = 1.0 / (x_cells * y_cells * z_freqs)
    potential = None
    for c, back in enumerate(z_weight(planes, greens, cas_m, chunks)):
        back = exchange(back, "gz")
        returned = [x_inverse(back, cas_x, p_me, s, pencils) for s in range(pencils)]
        returned = [shift(a, "pa", s) if s else a for s, a in enumerate(returned)]
        first = c * (z_slab // chunks)
        potential = y_inverse(returned, cas_y, p_me, scale, potential, z_slab, first)
    return potential


MESH = pl.DeviceIdType.MESH
HALVES = 2


def fits(density, green, groups, pencils):
    zs, xl, y = density.shape
    kb, yl, u = green.shape
    power = all(v & (v - 1) == 0 for v in (y, kb * groups, groups))
    rows = yl // groups // HALVES
    return (
        power
        and groups > 1
        and pencils > 1
        and u == y
        and xl * pencils == u
        and yl * pencils == y
        and rows % 16 == 0
        and u % 512 == 0
        and xl % 128 == 0
        and (yl // HALVES) % 128 == 0
        and kb >= zs
    )


def cas_of(product, length):
    angle = (product & (length - 1)).astype(F32) * (2.0 * math.pi / length)
    return jnp.cos(angle) + jnp.sin(angle)


def spectral(density, green, groups, pencils):
    n, pens = groups, pencils
    zs, xl, y = density.shape
    kb, yl, u = green.shape
    z_all, k_all = zs * n, kb * n
    half = yl // HALVES
    rows = half // n
    lanes = 512
    strip = 32

    def kernel(d_hbm, g_hbm, ret, t_out, dens, stage, gsend, grecv, ysend, yrecv, psend, precv,
               brecv, xsend, table, wide, tall, load, gs, gr, ys, yr, ps, pr, bs, br, xs, xr, own):
        g = lax.axis_index("gz")
        p = lax.axis_index("pa")

        def gz_at(i):
            return lax.rem(g + 1 + lax.rem(i + n // 2 - 1, n - 1), n)

        def pa_at(i):
            return lax.rem(p + 1 + i, pens)

        def green_load(t):
            h, i = t // n, lax.rem(t, n)
            d = lax.rem(jnp.where(i < n - 1, gz_at(i), g), n)
            at = pl.multiple_of(h * half + d * rows, rows)
            return pltpu.make_async_copy(
                g_hbm.at[:, pl.ds(at, rows), :], stage.at[lax.rem(t, 2)], load.at[lax.rem(t, 2)]
            )

        def green_send(h, d):
            return pltpu.make_async_remote_copy(
                gsend.at[h, d], grecv.at[h, g], gs.at[h, d], gr.at[h, g],
                device_id={"gz": d}, device_id_type=MESH)

        def green_wait(h, s):
            pltpu.make_async_remote_copy(
                gsend.at[h, s], grecv.at[h, s], gs.at[h, s], gr.at[h, s],
                device_id={"gz": s}, device_id_type=MESH).wait_recv()

        def y_copy(z, q, to):
            return pltpu.make_async_remote_copy(
                ysend.at[q, z], yrecv.at[to, z], ys.at[q, z], yr.at[to, z],
                device_id={"pa": q}, device_id_type=MESH)

        def p_copy(h, d, to):
            return pltpu.make_async_remote_copy(
                psend.at[h, d], precv.at[h, to], ps.at[h, d], pr.at[h, to],
                device_id={"gz": d}, device_id_type=MESH)

        def b_copy(h, z, d, to):
            return pltpu.make_async_remote_copy(
                gsend.at[h, d, z], brecv.at[h, z, to], bs.at[h, z, d], br.at[h, z, to],
                device_id={"gz": d}, device_id_type=MESH)

        def x_copy(h, z, q, to):
            at = pl.multiple_of(to * yl + h * half, half)
            return pltpu.make_async_remote_copy(
                xsend.at[h, z, q], ret.at[z, :, pl.ds(at, half)], xs.at[h, z, q], xr.at[h, z, to],
                device_id={"pa": q}, device_id_type=MESH)

        def x_own(h, z):
            at = pl.multiple_of(p * yl + h * half, half)
            return pltpu.make_async_copy(
                xsend.at[h, z, p], ret.at[z, :, pl.ds(at, half)], own.at[h, z])

        fill = pltpu.make_async_copy(d_hbm, dens, load.at[2])
        green_load(0).start()
        green_load(1).start()
        fill.start()
        barrier = pltpu.get_barrier_semaphore()

        @pl.loop(0, n - 1)
        def _(i):
            pl.semaphore_signal(barrier, inc=1, device_id={"gz": gz_at(i)}, device_id_type=MESH)

        @pl.loop(0, pens - 1)
        def _(i):
            pl.semaphore_signal(barrier, inc=1, device_id={"pa": pa_at(i)}, device_id_type=MESH)

        pl.semaphore_wait(barrier, n + pens - 2)

        @pl.loop(0, HALVES * n)
        def _(t):
            h, i = t // n, lax.rem(t, n)
            slot = lax.rem(t, 2)
            green_load(t).wait()

            @pl.when(i < n - 1)
            def _():
                d = gz_at(i)
                gsend[h, d] = stage[slot].astype(BF)
                green_send(h, d).start()

            @pl.when(i == n - 1)
            def _():
                grecv[h, g] = stage[slot].astype(BF)

            @pl.when(t < HALVES * n - 2)
            def _():
                green_load(t + 2).start()

        @pl.loop(0, y // strip)
        def _(b):
            row = lax.broadcasted_iota(jnp.int32, (strip, y), 0) + b * strip
            col = lax.broadcasted_iota(jnp.int32, (strip, y), 1)
            table[pl.ds(pl.multiple_of(b * strip, strip), strip), :] = cas_of(row * col, y).astype(BF)

        keep = pltpu.make_async_copy(table, t_out, load.at[3])
        keep.start()
        fill.wait()

        @pl.loop(0, zs)
        def _(z):
            for q in range(pens):
                ysend[q, z] = dot_t(table[q * yl : (q + 1) * yl, :], dens[z]).astype(BF)

            @pl.loop(0, pens - 1)
            def _(i):
                y_copy(z, pa_at(i), p).start()

            yrecv[p, z] = ysend[p, z]

        def widen(ref):
            shape = (strip, ref.shape[1])

            @pl.loop(0, ref.shape[0] // strip)
            def _(b):
                row = lax.broadcasted_iota(jnp.int32, shape, 0) + b * strip
                col = lax.broadcasted_iota(jnp.int32, shape, 1)
                value = cas_of((row >> 3) * (col >> 3), k_all)
                same = (row & 7) == (col & 7)
                ref[pl.ds(pl.multiple_of(b * strip, strip), strip), :] = jnp.where(same, value, 0.0).astype(BF)

        widen(wide)
        widen(tall)

        @pl.loop(0, zs)
        def _(z):
            @pl.loop(0, pens - 1)
            def _(i):
                s = pa_at(i)
                y_copy(z, s, s).wait_recv()

            total = dot(yrecv[0, z], table[0:xl, :])
            for q in range(1, pens):
                total += dot(yrecv[q, z], table[q * xl : (q + 1) * xl, :])
            total = total.astype(BF)
            for h in range(HALVES):
                for d in range(n):
                    at = h * half + d * rows
                    psend[h, d, z] = total[at : at + rows, :]

        for h in range(HALVES):
            @pl.loop(0, n - 1)
            def _(i):
                p_copy(h, gz_at(i), g).start()

            precv[h, g] = psend[h, g]

        for h in range(HALVES):
            @pl.loop(0, n - 1)
            def _(i):
                d = gz_at(i)
                green_send(h, d).wait_send()

        for h in range(HALVES):
            @pl.loop(0, n - 1)
            def _(i):
                s = gz_at(i)
                green_wait(h, s)
                p_copy(h, s, s).wait_recv()

            @pl.loop(0, u // lanes)
            def _(c):
                at = pl.ds(pl.multiple_of(c * lanes, lanes), lanes)
                for r in range(0, rows, 8):
                    part = slice(r, r + 8)
                    flat = precv[h, :, :, part, at].astype(F32).reshape(z_all * 8, lanes).astype(BF)
                    spec = dot(wide[...], flat)
                    weight = grecv[h, :, :, part, at].astype(F32).reshape(k_all * 8, lanes)
                    back = dot(tall[...], (spec * weight).astype(BF))
                    gsend[h, :, :zs, part, at] = back.reshape(n, zs, 8, lanes).astype(BF)

            @pl.loop(0, zs)
            def _(z):
                @pl.loop(0, n - 1)
                def _(i):
                    b_copy(h, z, gz_at(i), g).start()

                brecv[h, z, g] = gsend[h, g, z]

        @pl.loop(0, HALVES * zs)
        def _(t):
            h, z = t // zs, lax.rem(t, zs)

            @pl.loop(0, n - 1)
            def _(i):
                s = gz_at(i)
                b_copy(h, z, s, s).wait_recv()

            rows_in = brecv[h, z].reshape(half, u)
            for q in range(pens):
                xsend[h, z, q] = dot_t(table[q * xl : (q + 1) * xl, :], rows_in).astype(BF)

            @pl.loop(0, pens - 1)
            def _(i):
                x_copy(h, z, pa_at(i), p).start()

            x_own(h, z).start()

        keep.wait()

        @pl.loop(0, zs)
        def _(z):
            @pl.loop(0, pens - 1)
            def _(i):
                y_copy(z, pa_at(i), p).wait_send()

        @pl.loop(0, HALVES)
        def _(h):
            @pl.loop(0, n - 1)
            def _(i):
                p_copy(h, gz_at(i), g).wait_send()

        @pl.loop(0, HALVES * zs)
        def _(t):
            h, z = t // zs, lax.rem(t, zs)

            @pl.loop(0, n - 1)
            def _(i):
                b_copy(h, z, gz_at(i), g).wait_send()

            @pl.loop(0, pens - 1)
            def _(i):
                s = pa_at(i)
                x_copy(h, z, s, p).wait_send()
                x_copy(h, z, s, s).wait_recv()

            x_own(h, z).wait()

    sems = pltpu.SemaphoreType.DMA
    return pl.pallas_call(
        kernel,
        out_shape=[
            jax.ShapeDtypeStruct((zs, xl, y), BF),
            jax.ShapeDtypeStruct((y, y), BF),
        ],
        in_specs=[pl.BlockSpec(memory_space=pl.ANY)] * 2,
        out_specs=[pl.BlockSpec(memory_space=pl.ANY)] * 2,
        scratch_shapes=[
            pltpu.VMEM((zs, xl, y), BF),
            pltpu.VMEM((2, kb, rows, u), F32),
            pltpu.VMEM((HALVES, n, kb, rows, u), BF),
            pltpu.VMEM((HALVES, n, kb, rows, u), BF),
            pltpu.VMEM((pens, zs, yl, xl), BF),
            pltpu.VMEM((pens, zs, yl, xl), BF),
            pltpu.VMEM((HALVES, n, zs, rows, u), BF),
            pltpu.VMEM((HALVES, n, zs, rows, u), BF),
            pltpu.VMEM((HALVES, zs, n, rows, u), BF),
            pltpu.VMEM((HALVES, zs, pens, xl, half), BF),
            pltpu.VMEM((y, y), BF),
            pltpu.VMEM((k_all * 8, z_all * 8), BF),
            pltpu.VMEM((z_all * 8, k_all * 8), BF),
            sems((4,)),
            sems((HALVES, n)),
            sems((HALVES, n)),
            sems((pens, zs)),
            sems((pens, zs)),
            sems((HALVES, n)),
            sems((HALVES, n)),
            sems((HALVES, zs, n)),
            sems((HALVES, zs, n)),
            sems((HALVES, zs, pens)),
            sems((HALVES, zs, pens)),
            sems((HALVES, zs)),
        ],
        compiler_params=pltpu.CompilerParams(
            collective_id=0, has_side_effects=True, vmem_limit_bytes=67_000_000
        ),
        name="spectral",
    )(density, green)


def y_finish(returned, table, scale):
    z, x, y = returned.shape

    def body(r_ref, t_ref, o_ref):
        o_ref[0] = dot(r_ref[0], t_ref[...]) * scale

    return pl.pallas_call(
        body,
        grid=(z,),
        in_specs=[
            pl.BlockSpec((1, x, y), lambda i: (i, 0, 0)),
            pl.BlockSpec((y, y), lambda i: (0, 0)),
        ],
        out_specs=pl.BlockSpec((1, x, y), lambda i: (i, 0, 0)),
        out_shape=jax.ShapeDtypeStruct((z, x, y), F32),
        cost_estimate=cost(2 * z * x * y * y, returned, returned, returned),
        name="y_finish",
    )(returned, table)


def local(density, green):
    groups = lax.axis_size("gz")
    pencils = lax.axis_size("pa")
    if not fits(density, green, groups, pencils):
        return staged(density, green)
    scale = 1.0 / (green.shape[2] * density.shape[2] * green.shape[0] * groups)
    returned, table = spectral(density, green, groups, pencils)
    return y_finish(returned, table, scale)


def solution(mesh):
    return jax.shard_map(
        local,
        mesh=mesh,
        in_specs=(P("gz", "pa", None), P("gz", "pa", None)),
        out_specs=P("gz", "pa", None),
        check_vma=False,
    )
```

profile of v0, /device:TPU:13, one launch (start us, length us, event | category | flops | bytes accessed | tf_op | source)
XLA Modules:
  0.0 386.0 jit_solution(14641496244911755378)
XLA Ops:
  0.0 375.2 %spectral.1 = (bf16[8,256,1024]{2,1,0:T(8,128)(2,1)}, bf16[1024,1024]{1,0:T(8,128)(2,1)}) custom-call(bf16[8,256,1024]{2,1,0:T(8,128)(2,1)} %d_hbm.1, f32[16,256,1024]{2,1,0:T(8,128)} %g_hbm.1), custom_call_target="tpu_custom_call" | custom-call | tf_op jit(solution)/shard_map/spectral/pallas_call | solution.py:556
  375.3 10.7 %y_finish.1 = f32[8,256,1024]{2,1,0:T(8,128)} custom-call(bf16[8,256,1024]{2,1,0:T(8,128)(2,1)} %get-tuple-element.7.r_ref, bf16[1024,1024]{1,0:T(8,128)(2,1)} %get-tuple-element.8.t_ref), custom_call_target="tpu_custom_call" | custom-call | flops 4294967296 | bytes 12582912 | tf_op jit(solution)/shard_map/y_finish/pallas_call | solution.py:604
where the time goes:
time: 390 us; the launch traced here: 386 us
  Pallas kernels  386 us (99%)
    pallas_call x1, Pallas kernels, spectral(): pl.pallas_call(kernel, out_shape=[jax.ShapeDtypeStruct((zs, xl, y), BF),...  375 us
    pallas_call x1, Pallas kernels, y_finish(): pl.pallas_call(body, grid=(z,), in_specs=[pl.BlockSpec((1, x, y), lambda...  10.7 us

commit v1 on v0

--- a/solution.py
+++ b/solution.py
@@ -285,6 +285,7 @@
 
 MESH = pl.DeviceIdType.MESH
 HALVES = 2
+LATE = 2
 
 
 def fits(density, green, groups, pencils):
@@ -312,7 +313,7 @@
     return jnp.cos(angle) + jnp.sin(angle)
 
 
-def spectral(density, green, groups, pencils):
+def spectral(density, green, groups, pencils, scale):
     n, pens = groups, pencils
     zs, xl, y = density.shape
     kb, yl, u = green.shape
@@ -322,60 +323,88 @@
     lanes = 512
     strip = 32
 
-    def kernel(d_hbm, g_hbm, ret, t_out, dens, stage, gsend, grecv, ysend, yrecv, psend, precv,
-               brecv, xsend, table, wide, tall, load, gs, gr, ys, yr, ps, pr, bs, br, xs, xr, own):
+    early = max(zs - LATE, 0)
+
+    def kernel(d_hbm, g_hbm, out, t_out, dens, stage, gsend, grecv, ysend, yrecv, psend, precv,
+               brecv, xsend, ret, ready, table, wide, tall, load, gs, gr, ys, yr, ps, pr, bs, br, xs, xr,
+               own, done):
         g = lax.axis_index("gz")
         p = lax.axis_index("pa")
 
         def gz_at(i):
-            return lax.rem(g + 1 + lax.rem(i + n // 2 - 1, n - 1), n)
+            return lax.rem(g + 1 + i, n)
 
         def pa_at(i):
             return lax.rem(p + 1 + i, pens)
 
         def green_load(t):
             h, i = t // n, lax.rem(t, n)
-            d = lax.rem(jnp.where(i < n - 1, gz_at(i), g), n)
-            at = pl.multiple_of(h * half + d * rows, rows)
+            at = pl.multiple_of(h * half + gz_at(i) * rows, rows)
             return pltpu.make_async_copy(
                 g_hbm.at[:, pl.ds(at, rows), :], stage.at[lax.rem(t, 2)], load.at[lax.rem(t, 2)]
             )
 
-        def green_send(h, d):
+        def green_cast(t):
+            h, i = t // n, lax.rem(t, n)
+            slot = lax.rem(t, 2)
+            green_load(t).wait()
+
+            @pl.when(i < n - 1)
+            def _():
+                gsend[h, gz_at(i)] = stage[slot].astype(BF)
+
+            @pl.when(i == n - 1)
+            def _():
+                grecv[h, g] = stage[slot].astype(BF)
+
+            @pl.when(t < HALVES * n - 2)
+            def _():
+                green_load(t + 2).start()
+
+        def settle(ref, sem):
+            pltpu.make_async_copy(ref, ref, sem).wait()
+
+        def green_copy(h, d):
             return pltpu.make_async_remote_copy(
-                gsend.at[h, d], grecv.at[h, g], gs.at[h, d], gr.at[h, g],
+                gsend.at[h, d], grecv.at[h, g], gs, gr.at[h],
                 device_id={"gz": d}, device_id_type=MESH)
 
-        def green_wait(h, s):
-            pltpu.make_async_remote_copy(
-                gsend.at[h, s], grecv.at[h, s], gs.at[h, s], gr.at[h, s],
-                device_id={"gz": s}, device_id_type=MESH).wait_recv()
-
-        def y_copy(z, q, to):
+        def y_copy(z, q):
             return pltpu.make_async_remote_copy(
-                ysend.at[q, z], yrecv.at[to, z], ys.at[q, z], yr.at[to, z],
+                ysend.at[q, z], yrecv.at[p, z], ys, yr.at[z],
                 device_id={"pa": q}, device_id_type=MESH)
 
-        def p_copy(h, d, to):
+        def p_copy(h, d):
             return pltpu.make_async_remote_copy(
-                psend.at[h, d], precv.at[h, to], ps.at[h, d], pr.at[h, to],
+                psend.at[h, d], precv.at[h, g], ps, pr.at[h],
                 device_id={"gz": d}, device_id_type=MESH)
 
-        def b_copy(h, z, d, to):
+        def b_copy(h, z, d):
             return pltpu.make_async_remote_copy(
-                gsend.at[h, d, z], brecv.at[h, z, to], bs.at[h, z, d], br.at[h, z, to],
+                gsend.at[h, d, z], brecv.at[h, z, g], bs, br.at[h, z],
                 device_id={"gz": d}, device_id_type=MESH)
 
+        def x_at(h):
+            return pl.ds(pl.multiple_of(p * yl + h * half, half), half)
+
         def x_copy(h, z, q, to):
-            at = pl.multiple_of(to * yl + h * half, half)
             return pltpu.make_async_remote_copy(
-                xsend.at[h, z, q], ret.at[z, :, pl.ds(at, half)], xs.at[h, z, q], xr.at[h, z, to],
+                xsend.at[h, z, q], to.at[z, :, x_at(h)], xs, xr.at[z],
                 device_id={"pa": q}, device_id_type=MESH)
 
         def x_own(h, z):
-            at = pl.multiple_of(p * yl + h * half, half)
-            return pltpu.make_async_copy(
-                xsend.at[h, z, p], ret.at[z, :, pl.ds(at, half)], own.at[h, z])
+            return pltpu.make_async_copy(xsend.at[h, z, p], out.at[z, :, x_at(h)], own.at[h, z - early])
+
+        def y_back(z):
+            settle(ret.at[z, :, 0 : (pens - 1) * yl], xr.at[z])
+            slot = lax.rem(z, 2)
+
+            @pl.when(z >= 2)
+            def _():
+                settle(ready.at[slot], done.at[slot])
+
+            ready[slot] = (dot(ret[z], table[...]) * scale).astype(BF)
+            pltpu.make_async_copy(ready.at[slot], out.at[z], done.at[slot]).start()
 
         fill = pltpu.make_async_copy(d_hbm, dens, load.at[2])
         green_load(0).start()
@@ -391,27 +420,20 @@
         def _(i):
             pl.semaphore_signal(barrier, inc=1, device_id={"pa": pa_at(i)}, device_id_type=MESH)
 
+        green_cast(jnp.int32(0))
         pl.semaphore_wait(barrier, n + pens - 2)
 
         @pl.loop(0, HALVES * n)
         def _(t):
             h, i = t // n, lax.rem(t, n)
-            slot = lax.rem(t, 2)
-            green_load(t).wait()
 
             @pl.when(i < n - 1)
             def _():
-                d = gz_at(i)
-                gsend[h, d] = stage[slot].astype(BF)
-                green_send(h, d).start()
-
-            @pl.when(i == n - 1)
-            def _():
-                grecv[h, g] = stage[slot].astype(BF)
-
-            @pl.when(t < HALVES * n - 2)
-            def _():
-                green_load(t + 2).start()
+                green_copy(h, gz_at(i)).start()
+
+            @pl.when(t < HALVES * n - 1)
+            def _():
+                green_cast(t + 1)
 
         @pl.loop(0, y // strip)
         def _(b):
@@ -430,7 +452,7 @@
 
             @pl.loop(0, pens - 1)
             def _(i):
-                y_copy(z, pa_at(i), p).start()
+                y_copy(z, pa_at(i)).start()
 
             yrecv[p, z] = ysend[p, z]
 
@@ -450,10 +472,7 @@
 
         @pl.loop(0, zs)
         def _(z):
-            @pl.loop(0, pens - 1)
-            def _(i):
-                s = pa_at(i)
-                y_copy(z, s, s).wait_recv()
+            settle(yrecv.at[0 : pens - 1, z], yr.at[z])
 
             total = dot(yrecv[0, z], table[0:xl, :])
             for q in range(1, pens):
@@ -467,22 +486,14 @@
         for h in range(HALVES):
             @pl.loop(0, n - 1)
             def _(i):
-                p_copy(h, gz_at(i), g).start()
+                p_copy(h, gz_at(i)).start()
 
             precv[h, g] = psend[h, g]
 
+        settle(gsend.at[:, 0 : n - 1], gs)
         for h in range(HALVES):
-            @pl.loop(0, n - 1)
-            def _(i):
-                d = gz_at(i)
-                green_send(h, d).wait_send()
-
-        for h in range(HALVES):
-            @pl.loop(0, n - 1)
-            def _(i):
-                s = gz_at(i)
-                green_wait(h, s)
-                p_copy(h, s, s).wait_recv()
+            settle(grecv.at[h, 0 : n - 1], gr.at[h])
+            settle(precv.at[h, 0 : n - 1], pr.at[h])
 
             @pl.loop(0, u // lanes)
             def _(c):
@@ -499,58 +510,49 @@
             def _(z):
                 @pl.loop(0, n - 1)
                 def _(i):
-                    b_copy(h, z, gz_at(i), g).start()
+                    b_copy(h, z, gz_at(i)).start()
 
                 brecv[h, z, g] = gsend[h, g, z]
 
         @pl.loop(0, HALVES * zs)
         def _(t):
             h, z = t // zs, lax.rem(t, zs)
-
-            @pl.loop(0, n - 1)
-            def _(i):
-                s = gz_at(i)
-                b_copy(h, z, s, s).wait_recv()
-
+            settle(brecv.at[h, z, 0 : n - 1], br.at[h, z])
             rows_in = brecv[h, z].reshape(half, u)
             for q in range(pens):
                 xsend[h, z, q] = dot_t(table[q * xl : (q + 1) * xl, :], rows_in).astype(BF)
 
-            @pl.loop(0, pens - 1)
-            def _(i):
-                x_copy(h, z, pa_at(i), p).start()
-
-            x_own(h, z).start()
+            @pl.when(z < early)
+            def _():
+                @pl.loop(0, pens - 1)
+                def _(i):
+                    x_copy(h, z, pa_at(i), ret).start()
+
+                ret[z, :, x_at(h)] = xsend[h, z, p]
+
+            @pl.when(z >= early)
+            def _():
+                @pl.loop(0, pens - 1)
+                def _(i):
+                    x_copy(h, z, pa_at(i), out).start()
+
+                x_own(h, z).start()
+
+            @pl.when((h == HALVES - 1) & (z >= LATE))
+            def _():
+                y_back(z - LATE)
 
         keep.wait()
-
-        @pl.loop(0, zs)
-        def _(z):
-            @pl.loop(0, pens - 1)
-            def _(i):
-                y_copy(z, pa_at(i), p).wait_send()
-
-        @pl.loop(0, HALVES)
-        def _(h):
-            @pl.loop(0, n - 1)
-            def _(i):
-                p_copy(h, gz_at(i), g).wait_send()
-
-        @pl.loop(0, HALVES * zs)
-        def _(t):
-            h, z = t // zs, lax.rem(t, zs)
-
-            @pl.loop(0, n - 1)
-            def _(i):
-                b_copy(h, z, gz_at(i), g).wait_send()
-
-            @pl.loop(0, pens - 1)
-            def _(i):
-                s = pa_at(i)
-                x_copy(h, z, s, p).wait_send()
-                x_copy(h, z, s, s).wait_recv()
-
-            x_own(h, z).wait()
+        settle(ysend.at[0 : pens - 1], ys)
+        settle(psend.at[:, 0 : n - 1], ps)
+        settle(gsend.at[:, 0 : n - 1, 0:zs], bs)
+        settle(xsend.at[:, :, 0 : pens - 1], xs)
+        for z in range(max(early - 2, 0), early):
+            settle(ready.at[z % 2], done.at[z % 2])
+        for z in range(early, zs):
+            for h in range(HALVES):
+                x_own(h, z).wait()
+            settle(out.at[z, :, 0 : (pens - 1) * yl], xr.at[z])
 
     sems = pltpu.SemaphoreType.DMA
     return pl.pallas_call(
@@ -572,21 +574,24 @@
             pltpu.VMEM((HALVES, n, zs, rows, u), BF),
             pltpu.VMEM((HALVES, zs, n, rows, u), BF),
             pltpu.VMEM((HALVES, zs, pens, xl, half), BF),
+            pltpu.VMEM((max(early, 1), xl, y), BF),
+            pltpu.VMEM((2, xl, y), BF),
             pltpu.VMEM((y, y), BF),
             pltpu.VMEM((k_all * 8, z_all * 8), BF),
             pltpu.VMEM((z_all * 8, k_all * 8), BF),
             sems((4,)),
-            sems((HALVES, n)),
-            sems((HALVES, n)),
-            sems((pens, zs)),
-            sems((pens, zs)),
-            sems((HALVES, n)),
-            sems((HALVES, n)),
-            sems((HALVES, zs, n)),
-            sems((HALVES, zs, n)),
-            sems((HALVES, zs, pens)),
-            sems((HALVES, zs, pens)),
+            sems,
+            sems((HALVES,)),
+            sems,
+            sems((zs,)),
+            sems,
+            sems((HALVES,)),
+            sems,
             sems((HALVES, zs)),
+            sems,
+            sems((zs,)),
+            sems((HALVES, zs - early)),
+            sems((2,)),
         ],
         compiler_params=pltpu.CompilerParams(
             collective_id=0, has_side_effects=True, vmem_limit_bytes=67_000_000
@@ -595,24 +600,53 @@
     )(density, green)
 
 
-def y_finish(returned, table, scale):
-    z, x, y = returned.shape
-
-    def body(r_ref, t_ref, o_ref):
-        o_ref[0] = dot(r_ref[0], t_ref[...]) * scale
-
+def y_finish(mixed, table, scale):
+    z, x, y = mixed.shape
+    early = max(z - LATE, 0)
+    order = [*range(early - early // 4), *range(early, z), *range(early - early // 4, early)]
+
+    def body(m_hbm, t_hbm, o_hbm, held, table, made, fill, arrive, leave):
+        def taken(i):
+            return pltpu.make_async_copy(m_hbm.at[i], held.at[i], arrive.at[i])
+
+        def given(i):
+            return pltpu.make_async_copy(made.at[i], o_hbm.at[i], leave.at[i])
+
+        lookup = pltpu.make_async_copy(t_hbm, table, fill)
+        for at, i in enumerate(order):
+            taken(i).start()
+            if at == 0:
+                lookup.start()
+        for i in order:
+            if i == early:
+                lookup.wait()
+            taken(i).wait()
+            if i < early:
+                made[i] = held[i].astype(F32)
+            else:
+                made[i] = dot(held[i], table[...]) * scale
+            given(i).start()
+        for i in order:
+            given(i).wait()
+
+    sems = pltpu.SemaphoreType.DMA
     return pl.pallas_call(
         body,
-        grid=(z,),
-        in_specs=[
-            pl.BlockSpec((1, x, y), lambda i: (i, 0, 0)),
-            pl.BlockSpec((y, y), lambda i: (0, 0)),
+        in_specs=[pl.BlockSpec(memory_space=pl.ANY)] * 2,
+        out_specs=pl.BlockSpec(memory_space=pl.ANY),
+        out_shape=jax.ShapeDtypeStruct((z, x, y), F32),
+        scratch_shapes=[
+            pltpu.VMEM((z, x, y), BF),
+            pltpu.VMEM((y, y), BF),
+            pltpu.VMEM((z, x, y), F32),
+            sems,
+            sems((z,)),
+            sems((z,)),
         ],
-        out_specs=pl.BlockSpec((1, x, y), lambda i: (i, 0, 0)),
-        out_shape=jax.ShapeDtypeStruct((z, x, y), F32),
-        cost_estimate=cost(2 * z * x * y * y, returned, returned, returned),
+        cost_estimate=cost(2 * LATE * x * y * y, mixed, mixed, mixed),
+        compiler_params=pltpu.CompilerParams(vmem_limit_bytes=67_000_000),
         name="y_finish",
-    )(returned, table)
+    )(mixed, table)
 
 
 def local(density, green):
@@ -621,8 +655,8 @@
     if not fits(density, green, groups, pencils):
         return staged(density, green)
     scale = 1.0 / (green.shape[2] * density.shape[2] * green.shape[0] * groups)
-    returned, table = spectral(density, green, groups, pencils)
-    return y_finish(returned, table, scale)
+    mixed, table = spectral(density, green, groups, pencils, scale)
+    return y_finish(mixed, table, scale)
 
 
 def solution(mesh):

time: 390 us -> 380 us (0.974); the launches traced: 386 us -> 380 us
  Pallas kernels: 386 us -> 380 us
where the time goes in v1:
time: 380 us
  Pallas kernels  380 us (100%)
    pallas_call x1, Pallas kernels, spectral(): pl.pallas_call(kernel, out_shape=[jax.ShapeDtypeStruct((zs, xl, y), BF),...  373 us

profile of v1, /device:TPU:13, one launch (start us, length us, event | category | flops | bytes accessed | tf_op | source)
XLA Modules:
  0.0 380.1 jit_solution(14794658485447692097)
XLA Ops:
  0.0 373.0 %spectral.1 = (bf16[8,256,1024]{2,1,0:T(8,128)(2,1)}, bf16[1024,1024]{1,0:T(8,128)(2,1)}) custom-call(bf16[8,256,1024]{2,1,0:T(8,128)(2,1)} %d_hbm.1, f32[16,256,1024]{2,1,0:T(8,128)} %g_hbm.1), custom_call_target="tpu_custom_call" | custom-call | tf_op jit(solution)/shard_map/spectral/pallas_call | solution.py:558
  373.0 7.1 %y_finish.1 = f32[8,256,1024]{2,1,0:T(8,128)} custom-call(bf16[8,256,1024]{2,1,0:T(8,128)(2,1)} %get-tuple-element.7.m_hbm, bf16[1024,1024]{1,0:T(8,128)(2,1)} %get-tuple-element.8.t_hbm), custom_call_target="tpu_custom_call" | custom-call | flops 1073741824 | bytes 12582912 | tf_op jit(solution)/shard_map/y_finish/pallas_call | solution.py:633

commit v2 on v1

--- a/solution.py
+++ b/solution.py
@@ -285,7 +285,7 @@
 
 MESH = pl.DeviceIdType.MESH
 HALVES = 2
-LATE = 2
+LAG = 2
 
 
 def fits(density, green, groups, pencils):
@@ -323,11 +323,12 @@
     lanes = 512
     strip = 32
 
-    early = max(zs - LATE, 0)
-
-    def kernel(d_hbm, g_hbm, out, t_out, dens, stage, gsend, grecv, ysend, yrecv, psend, precv,
+    lag = min(LAG, zs)
+    others = [*range(1, pens - 1), 0] if pens > 2 else [0]
+
+    def kernel(d_hbm, g_hbm, out, dens, stage, gsend, grecv, ysend, yrecv, psend, precv,
                brecv, xsend, ret, ready, table, wide, tall, load, gs, gr, ys, yr, ps, pr, bs, br, xs, xr,
-               own, done):
+               done):
         g = lax.axis_index("gz")
         p = lax.axis_index("pa")
 
@@ -387,13 +388,10 @@
         def x_at(h):
             return pl.ds(pl.multiple_of(p * yl + h * half, half), half)
 
-        def x_copy(h, z, q, to):
+        def x_copy(h, z, q):
             return pltpu.make_async_remote_copy(
-                xsend.at[h, z, q], to.at[z, :, x_at(h)], xs, xr.at[z],
+                xsend.at[h, z, q], ret.at[z, :, x_at(h)], xs, xr.at[z],
                 device_id={"pa": q}, device_id_type=MESH)
-
-        def x_own(h, z):
-            return pltpu.make_async_copy(xsend.at[h, z, p], out.at[z, :, x_at(h)], own.at[h, z - early])
 
         def y_back(z):
             settle(ret.at[z, :, 0 : (pens - 1) * yl], xr.at[z])
@@ -441,8 +439,6 @@
             col = lax.broadcasted_iota(jnp.int32, (strip, y), 1)
             table[pl.ds(pl.multiple_of(b * strip, strip), strip), :] = cas_of(row * col, y).astype(BF)
 
-        keep = pltpu.make_async_copy(table, t_out, load.at[3])
-        keep.start()
         fill.wait()
 
         @pl.loop(0, zs)
@@ -519,50 +515,37 @@
             h, z = t // zs, lax.rem(t, zs)
             settle(brecv.at[h, z, 0 : n - 1], br.at[h, z])
             rows_in = brecv[h, z].reshape(half, u)
-            for q in range(pens):
-                xsend[h, z, q] = dot_t(table[q * xl : (q + 1) * xl, :], rows_in).astype(BF)
-
-            @pl.when(z < early)
+
+            def piece(q):
+                at = pl.ds(pl.multiple_of(q * xl, xl), xl)
+                return dot_t(table[at, :], rows_in).astype(BF)
+
+            for at, i in enumerate(others):
+                xsend[h, z, pa_at(i)] = piece(pa_at(i))
+                if at:
+                    x_copy(h, z, pa_at(others[at - 1])).start()
+            ret[z, :, x_at(h)] = piece(p)
+            x_copy(h, z, pa_at(others[-1])).start()
+
+            @pl.when((h == HALVES - 1) & (z >= lag))
             def _():
-                @pl.loop(0, pens - 1)
-                def _(i):
-                    x_copy(h, z, pa_at(i), ret).start()
-
-                ret[z, :, x_at(h)] = xsend[h, z, p]
-
-            @pl.when(z >= early)
-            def _():
-                @pl.loop(0, pens - 1)
-                def _(i):
-                    x_copy(h, z, pa_at(i), out).start()
-
-                x_own(h, z).start()
-
-            @pl.when((h == HALVES - 1) & (z >= LATE))
-            def _():
-                y_back(z - LATE)
-
-        keep.wait()
+                y_back(z - lag)
+
+        for z in range(zs - lag, zs):
+            y_back(jnp.int32(z))
         settle(ysend.at[0 : pens - 1], ys)
         settle(psend.at[:, 0 : n - 1], ps)
         settle(gsend.at[:, 0 : n - 1, 0:zs], bs)
         settle(xsend.at[:, :, 0 : pens - 1], xs)
-        for z in range(max(early - 2, 0), early):
+        for z in range(max(zs - 2, 0), zs):
             settle(ready.at[z % 2], done.at[z % 2])
-        for z in range(early, zs):
-            for h in range(HALVES):
-                x_own(h, z).wait()
-            settle(out.at[z, :, 0 : (pens - 1) * yl], xr.at[z])
 
     sems = pltpu.SemaphoreType.DMA
     return pl.pallas_call(
         kernel,
-        out_shape=[
-            jax.ShapeDtypeStruct((zs, xl, y), BF),
-            jax.ShapeDtypeStruct((y, y), BF),
-        ],
+        out_shape=jax.ShapeDtypeStruct((zs, xl, y), BF),
         in_specs=[pl.BlockSpec(memory_space=pl.ANY)] * 2,
-        out_specs=[pl.BlockSpec(memory_space=pl.ANY)] * 2,
+        out_specs=pl.BlockSpec(memory_space=pl.ANY),
         scratch_shapes=[
             pltpu.VMEM((zs, xl, y), BF),
             pltpu.VMEM((2, kb, rows, u), F32),
@@ -574,12 +557,12 @@
             pltpu.VMEM((HALVES, n, zs, rows, u), BF),
             pltpu.VMEM((HALVES, zs, n, rows, u), BF),
             pltpu.VMEM((HALVES, zs, pens, xl, half), BF),
-            pltpu.VMEM((max(early, 1), xl, y), BF),
+            pltpu.VMEM((zs, xl, y), BF),
             pltpu.VMEM((2, xl, y), BF),
             pltpu.VMEM((y, y), BF),
             pltpu.VMEM((k_all * 8, z_all * 8), BF),
             pltpu.VMEM((z_all * 8, k_all * 8), BF),
-            sems((4,)),
+            sems((3,)),
             sems,
             sems((HALVES,)),
             sems,
@@ -590,7 +573,6 @@
             sems((HALVES, zs)),
             sems,
             sems((zs,)),
-            sems((HALVES, zs - early)),
             sems((2,)),
         ],
         compiler_params=pltpu.CompilerParams(
@@ -600,53 +582,41 @@
     )(density, green)
 
 
-def y_finish(mixed, table, scale):
-    z, x, y = mixed.shape
-    early = max(z - LATE, 0)
-    order = [*range(early - early // 4), *range(early, z), *range(early - early // 4, early)]
-
-    def body(m_hbm, t_hbm, o_hbm, held, table, made, fill, arrive, leave):
+def widen_result(narrow):
+    z, x, y = narrow.shape
+
+    def body(n_hbm, o_hbm, held, made, arrive, leave):
         def taken(i):
-            return pltpu.make_async_copy(m_hbm.at[i], held.at[i], arrive.at[i])
+            return pltpu.make_async_copy(n_hbm.at[i], held.at[i], arrive.at[i])
 
         def given(i):
             return pltpu.make_async_copy(made.at[i], o_hbm.at[i], leave.at[i])
 
-        lookup = pltpu.make_async_copy(t_hbm, table, fill)
-        for at, i in enumerate(order):
+        for i in range(z):
             taken(i).start()
-            if at == 0:
-                lookup.start()
-        for i in order:
-            if i == early:
-                lookup.wait()
+        for i in range(z):
             taken(i).wait()
-            if i < early:
-                made[i] = held[i].astype(F32)
-            else:
-                made[i] = dot(held[i], table[...]) * scale
+            made[i] = held[i].astype(F32)
             given(i).start()
-        for i in order:
+        for i in range(z):
             given(i).wait()
 
     sems = pltpu.SemaphoreType.DMA
     return pl.pallas_call(
         body,
-        in_specs=[pl.BlockSpec(memory_space=pl.ANY)] * 2,
+        in_specs=[pl.BlockSpec(memory_space=pl.ANY)],
         out_specs=pl.BlockSpec(memory_space=pl.ANY),
         out_shape=jax.ShapeDtypeStruct((z, x, y), F32),
         scratch_shapes=[
             pltpu.VMEM((z, x, y), BF),
-            pltpu.VMEM((y, y), BF),
             pltpu.VMEM((z, x, y), F32),
-            sems,
             sems((z,)),
             sems((z,)),
         ],
-        cost_estimate=cost(2 * LATE * x * y * y, mixed, mixed, mixed),
         compiler_params=pltpu.CompilerParams(vmem_limit_bytes=67_000_000),
-        name="y_finish",
-    )(mixed, table)
+        cost_estimate=cost(z * x * y, narrow, narrow, narrow),
+        name="widen_result",
+    )(narrow)
 
 
 def local(density, green):
@@ -655,8 +625,7 @@
     if not fits(density, green, groups, pencils):
         return staged(density, green)
     scale = 1.0 / (green.shape[2] * density.shape[2] * green.shape[0] * groups)
-    mixed, table = spectral(density, green, groups, pencils, scale)
-    return y_finish(mixed, table, scale)
+    return widen_result(spectral(density, green, groups, pencils, scale))
 
 
 def solution(mesh):

time: 380 us -> 379 us (level)
  no operation moved by 1% of the time
where the time goes in v2:
time: 379 us
  Pallas kernels  379 us (100%)
    pallas_call x1, Pallas kernels, spectral(): pl.pallas_call(kernel, out_shape=jax.ShapeDtypeStruct((zs, xl, y), BF), i...  374 us

profile of v2, /device:TPU:13, one launch (start us, length us, event | category | flops | bytes accessed | tf_op | source)
XLA Modules:
  0.0 378.7 jit_solution(6008774280724782066)
XLA Ops:
  0.0 374.2 %spectral.1.n_hbm = bf16[8,256,1024]{2,1,0:T(8,128)(2,1)} custom-call(bf16[8,256,1024]{2,1,0:T(8,128)(2,1)} %d_hbm.1, f32[16,256,1024]{2,1,0:T(8,128)} %g_hbm.1), custom_call_target="tpu_custom_call" | custom-call | tf_op jit(solution)/shard_map/spectral/pallas_call | solution.py:544
  374.2 4.5 %widen_result.1 = f32[8,256,1024]{2,1,0:T(8,128)} custom-call(bf16[8,256,1024]{2,1,0:T(8,128)(2,1)} %spectral.1.n_hbm), custom_call_target="tpu_custom_call" | custom-call | flops 2097152 | bytes 12582912 | tf_op jit(solution)/shard_map/widen_result/pallas_call | solution.py:605

commit v3 on v2

--- a/solution.py
+++ b/solution.py
@@ -401,8 +401,10 @@
             def _():
                 settle(ready.at[slot], done.at[slot])
 
-            ready[slot] = (dot(ret[z], table[...]) * scale).astype(BF)
-            pltpu.make_async_copy(ready.at[slot], out.at[z], done.at[slot]).start()
+            for at in range(0, xl, xl // 2):
+                part = slice(at, at + xl // 2)
+                ready[slot, part] = (dot(ret[z, part], table[...]) * scale).astype(BF)
+                pltpu.make_async_copy(ready.at[slot, part], out.at[z, part], done.at[slot]).start()
 
         fill = pltpu.make_async_copy(d_hbm, dens, load.at[2])
         green_load(0).start()

time: 379 us -> 379 us (level)
  no operation moved by 1% of the time
where the time goes in v3:
time: 379 us
  Pallas kernels  379 us (100%)
    pallas_call x1, Pallas kernels, spectral(): pl.pallas_call(kernel, out_shape=jax.ShapeDtypeStruct((zs, xl, y), BF), i...  374 us

profile of v3, /device:TPU:13, one launch (start us, length us, event | category | flops | bytes accessed | tf_op | source)
XLA Modules:
  0.0 378.7 jit_solution(14811095672382867500)
XLA Ops:
  0.0 374.1 %spectral.1.n_hbm = bf16[8,256,1024]{2,1,0:T(8,128)(2,1)} custom-call(bf16[8,256,1024]{2,1,0:T(8,128)(2,1)} %d_hbm.1, f32[16,256,1024]{2,1,0:T(8,128)} %g_hbm.1), custom_call_target="tpu_custom_call" | custom-call | tf_op jit(solution)/shard_map/spectral/pallas_call | solution.py:546
  374.1 4.5 %widen_result.1 = f32[8,256,1024]{2,1,0:T(8,128)} custom-call(bf16[8,256,1024]{2,1,0:T(8,128)(2,1)} %spectral.1.n_hbm), custom_call_target="tpu_custom_call" | custom-call | flops 2097152 | bytes 12582912 | tf_op jit(solution)/shard_map/widen_result/pallas_call | solution.py:607
